TPU v7x, 32 devices: a whole 2x2x4 slice. The times are simulated.
32 devices in a mesh: dp: 4 (over z), row: 4 (over y, x), col: 2 (over core).
Axes of the slice: x: 2, y: 2, z: 4, core: 2. Of those that a mesh axis runs over, the one named last changes fastest.
Arguments:
- layer_input: bfloat16 [8192, 1536], P(('dp', 'row'), 'col'), may hold values from -6 to 6
- gain_attn: float32 [1536], P('col'), may hold values from 0.25 to 1.75
- gain_ffn: float32 [1536], P('col'), may hold values from 0.25 to 1.75
- w_query: bfloat16 [1536, 1536], P('col', 'row'), may hold values from -0.15625 to 0.15625
- w_key: bfloat16 [1536, 768], P('col', 'row'), may hold values from -0.15625 to 0.15625
- w_value: bfloat16 [1536, 768], P('col', 'row'), may hold values from -0.15625 to 0.15625
- w_out: bfloat16 [1536, 1536], P('row', 'col'), may hold values from -1.25 to 1.25
- w_gate: bfloat16 [1536, 4096], P('col', 'row'), may hold values from -0.15625 to 0.15625
- w_up: bfloat16 [1536, 4096], P('col', 'row'), may hold values from -0.15625 to 0.15625
- w_down: bfloat16 [4096, 1536], P('row', 'col'), may hold values from -0.09375 to 0.09375
- cotangent: bfloat16 [8192, 1536], P(('dp', 'row'), 'col'), may hold values from -6 to 6
Outputs:
- layer_output: float32 [8192, 1536], P(('dp', 'row'), 'col')
- grad_input: float32 [8192, 1536], P(('dp', 'row'), 'col')
- grad_gain_attn: float32 [1536], P('col')
- grad_gain_ffn: float32 [1536], P('col')
- grad_query: float32 [1536, 1536], P('col', 'row')
- grad_key: float32 [1536, 768], P('col', 'row')
- grad_value: float32 [1536, 768], P('col', 'row')
- grad_out: float32 [1536, 1536], P('row', 'col')
- grad_gate: float32 [1536, 4096], P('col', 'row')
- grad_up: float32 [1536, 4096], P('col', 'row')
- grad_down: float32 [4096, 1536], P('row', 'col')
All inputs are finite; a program needn't handle non-finite values.
Results may differ from a plain program's by a relative error of at most 0.014.
Values may be sent and summed in bfloat16 or wider, within the bound.
A program may use at most 192 MiB of HBM per device.

v0:
```python
import jax
import jax.numpy as jnp
from jax import lax
from jax.sharding import PartitionSpec as P

D = 1536
HD = 96
LENGTH = 1024
EPS = 1e-05
THETA = 100000.0


def rotate(values, heads, inverse):
    count = values.shape[0]
    half = HD // 2
    pos = (jnp.arange(count) % LENGTH).astype(jnp.float32)
    freq = THETA ** (-jnp.arange(half).astype(jnp.float32) * 2.0 / HD)
    angle = pos[:, None] * freq[None, :]
    cosine = jnp.cos(angle)[:, None, :]
    sine = jnp.sin(angle)[:, None, :]
    shaped = values.reshape(count, heads, HD)
    first = shaped[..., :half]
    second = shaped[..., half:]
    if inverse:
        joined = jnp.concatenate(
            [first * cosine + second * sine, second * cosine - first * sine], -1
        )
    else:
        joined = jnp.concatenate(
            [first * cosine - second * sine, second * cosine + first * sine], -1
        )
    return joined.reshape(count, heads * HD)


def masked_scores(query_block, keys_seq, block_index):
    rows = query_block.shape[0]
    span = keys_seq.shape[0]
    scores = jnp.einsum(
        "qkgd,skd->kgqs", query_block, keys_seq, preferred_element_type=jnp.float32
    ) * HD ** (-0.5)
    qpos = block_index * rows + jnp.arange(rows)
    allowed = jnp.arange(span)[None, :] <= qpos[:, None]
    return jnp.where(allowed[None, None], scores, -1e30)


def attend_forward(queries, keys, values, kv_heads):
    total = queries.shape[0]
    group = queries.shape[1] // (kv_heads * HD)
    block = min(512, LENGTH)
    count = LENGTH // block
    outputs = []
    sums = []
    for seq in range(total // LENGTH):
        start = seq * LENGTH
        keys_seq = keys[start : start + LENGTH].reshape(LENGTH, kv_heads, HD)
        vals_seq = values[start : start + LENGTH].reshape(LENGTH, kv_heads, HD)
        query_seq = queries[start : start + LENGTH].reshape(count, block, kv_heads, group, HD)

        def one_block(pair):
            query_block, index = pair
            scores = masked_scores(query_block, keys_seq, index)
            top = jnp.max(scores, -1, keepdims=True)
            expo = jnp.exp(scores - top)
            total_weight = jnp.sum(expo, -1, keepdims=True)
            probs = (expo / total_weight).astype(jnp.bfloat16)
            mixed = jnp.einsum(
                "kgqs,skd->qkgd", probs, vals_seq, preferred_element_type=jnp.float32
            )
            return (mixed.reshape(block, -1), (top + jnp.log(total_weight))[..., 0])

        mixed, logsum = lax.map(one_block, (query_seq, jnp.arange(count)))
        outputs.append(mixed.reshape(LENGTH, -1))
        sums.append(logsum)
    return (jnp.concatenate(outputs, 0), sums)


def attend_backward(queries, keys, values, grad_mixed, sums, kv_heads):
    total = queries.shape[0]
    group = queries.shape[1] // (kv_heads * HD)
    block = min(512, LENGTH)
    count = LENGTH // block
    scale = HD ** (-0.5)
    grad_q = []
    grad_k = []
    grad_v = []
    for seq in range(total // LENGTH):
        start = seq * LENGTH
        keys_seq = keys[start : start + LENGTH].reshape(LENGTH, kv_heads, HD)
        vals_seq = values[start : start + LENGTH].reshape(LENGTH, kv_heads, HD)
        query_seq = queries[start : start + LENGTH].reshape(count, block, kv_heads, group, HD)
        grad_seq = grad_mixed[start : start + LENGTH].reshape(count, block, kv_heads, group, HD)

        def one_block(carry, quad):
            key_acc, val_acc = carry
            query_block, grad_block, logsum, index = quad
            scores = masked_scores(query_block, keys_seq, index)
            probs = jnp.exp(scores - logsum[..., None])
            grad_probs = jnp.einsum(
                "qkgd,skd->kgqs", grad_block, vals_seq, preferred_element_type=jnp.float32
            )
            inner = jnp.sum(probs * grad_probs, -1, keepdims=True)
            grad_scores = (probs * (grad_probs - inner)).astype(jnp.bfloat16)
            dq_block = (
                jnp.einsum(
                    "kgqs,skd->qkgd", grad_scores, keys_seq, preferred_element_type=jnp.float32
                )
                * scale
            )
            key_acc = (
                key_acc
                + jnp.einsum(
                    "kgqs,qkgd->skd", grad_scores, query_block, preferred_element_type=jnp.float32
                )
                * scale
            )
            val_acc = val_acc + jnp.einsum(
                "kgqs,qkgd->skd",
                probs.astype(jnp.bfloat16),
                grad_block,
                preferred_element_type=jnp.float32,
            )
            return ((key_acc, val_acc), dq_block.reshape(block, -1))

        zero = jnp.zeros((LENGTH, kv_heads, HD), jnp.float32)
        (key_acc, val_acc), dq_seq = lax.scan(
            one_block, (zero, zero), (query_seq, grad_seq, sums[seq], jnp.arange(count))
        )
        grad_q.append(dq_seq.reshape(LENGTH, -1))
        grad_k.append(key_acc.reshape(LENGTH, -1))
        grad_v.append(val_acc.reshape(LENGTH, -1))
    return (jnp.concatenate(grad_q, 0), jnp.concatenate(grad_k, 0), jnp.concatenate(grad_v, 0))


def width_total(values):
    return lax.psum(values, "col")


def gather_tokens(values):
    return lax.all_gather(values, "row", axis=0, tiled=True)


def width_sum(values):
    return lax.psum(values, "col")


def token_sum(source, weight):
    return lax.psum_scatter(
        jnp.einsum("tj,jc->tc", source, weight, preferred_element_type=jnp.float32),
        "row",
        scatter_dimension=0,
        tiled=True,
    )


def on_device(
    layer_input,
    gain_attn,
    gain_ffn,
    w_query,
    w_key,
    w_value,
    w_out,
    w_gate,
    w_up,
    w_down,
    cotangent,
):
    input_f32 = layer_input.astype(jnp.float32)
    q_cols = w_query.shape[1]
    k_cols = w_key.shape[1]
    f_cols = w_gate.shape[1]
    w_in = jnp.concatenate([w_query, w_key, w_value], 1)
    w_gateup = jnp.concatenate([w_gate, w_up], 1)
    rstd1 = lax.rsqrt(width_total(jnp.sum(input_f32 * input_f32, 1)) / D + EPS)[:, None]
    normed_a = (input_f32 * rstd1 * gain_attn).astype(jnp.bfloat16)
    all_a = gather_tokens(normed_a)
    projected = width_sum(jnp.dot(all_a, w_in, preferred_element_type=jnp.float32))
    q_sum = projected[:, :q_cols]
    k_sum = projected[:, q_cols : q_cols + k_cols]
    v_sum = projected[:, q_cols + k_cols :]
    heads_q = q_sum.shape[1] // HD
    heads_k = k_sum.shape[1] // HD
    queries = rotate(q_sum, heads_q, False).astype(jnp.bfloat16)
    keys = rotate(k_sum, heads_k, False).astype(jnp.bfloat16)
    values = v_sum.astype(jnp.bfloat16)
    mixed, sums = attend_forward(queries, keys, values, heads_k)
    own_attn = mixed.astype(jnp.bfloat16)
    hidden = input_f32 + token_sum(own_attn, w_out)
    rstd2 = lax.rsqrt(width_total(jnp.sum(hidden * hidden, 1)) / D + EPS)[:, None]
    normed_f = (hidden * rstd2 * gain_ffn).astype(jnp.bfloat16)
    all_f = gather_tokens(normed_f)
    gateup_part = jnp.dot(all_f, w_gateup, preferred_element_type=jnp.float32)
    gateup = width_sum(gateup_part)
    gate = gateup[:, :f_cols]
    upper = gateup[:, f_cols:]
    sig = 1.0 / (1.0 + jnp.exp(-gate))
    own_middle = (gate * sig * upper).astype(jnp.bfloat16)
    layer_output = hidden + token_sum(own_middle, w_down)
    all_dy = gather_tokens(cotangent)
    gw_down = jnp.einsum("tf,tc->fc", own_middle, all_dy, preferred_element_type=jnp.float32)
    mid_part = jnp.einsum("tc,fc->tf", all_dy, w_down, preferred_element_type=jnp.float32)
    d_mid = width_sum(mid_part)
    d_gate = (d_mid * upper * sig * (1.0 + gate * (1.0 - sig))).astype(jnp.bfloat16)
    d_up = (d_mid * gate * sig).astype(jnp.bfloat16)
    d_gateup = jnp.concatenate([d_gate, d_up], 1)
    gw_gateup = jnp.einsum("tc,tf->cf", all_f, d_gateup, preferred_element_type=jnp.float32)
    d_nf = token_sum(d_gateup, w_gateup.T)
    part_gain_ffn = jnp.sum(d_nf * hidden * rstd2, 0)
    scaled2 = d_nf * gain_ffn
    inner2 = width_total(jnp.sum(scaled2 * hidden, 1))[:, None]
    d_hidden = cotangent.astype(jnp.float32) + rstd2 * scaled2 - hidden * rstd2**3 * inner2 / D
    all_dya = gather_tokens(d_hidden.astype(jnp.bfloat16))
    gw_out = jnp.einsum("tq,tc->qc", own_attn, all_dya, preferred_element_type=jnp.float32)
    attn_part = jnp.einsum("tc,qc->tq", all_dya, w_out, preferred_element_type=jnp.float32)
    d_attn = width_sum(attn_part).astype(jnp.bfloat16)
    dq_rot, dk_rot, dv = attend_backward(queries, keys, values, d_attn, sums, heads_k)
    d_q = rotate(dq_rot, heads_q, True).astype(jnp.bfloat16)
    d_k = rotate(dk_rot, heads_k, True).astype(jnp.bfloat16)
    d_v = dv.astype(jnp.bfloat16)
    d_proj = jnp.concatenate([d_q, d_k, d_v], 1)
    gw_in = jnp.einsum("tc,tj->cj", all_a, d_proj, preferred_element_type=jnp.float32)
    sum_down, sum_gateup, sum_in, sum_out = lax.psum((gw_down, gw_gateup, gw_in, gw_out), "dp")
    d_na = token_sum(d_proj, w_in.T)
    part_gain_attn = jnp.sum(d_na * input_f32 * rstd1, 0)
    scaled1 = d_na * gain_attn
    inner1 = width_total(jnp.sum(scaled1 * input_f32, 1))[:, None]
    grad_input = d_hidden + rstd1 * scaled1 - input_f32 * rstd1**3 * inner1 / D
    gain_a, gain_f = lax.psum((part_gain_attn, part_gain_ffn), ("dp", "row"))
    return (
        layer_output,
        grad_input,
        gain_a,
        gain_f,
        sum_in[:, :q_cols],
        sum_in[:, q_cols : q_cols + k_cols],
        sum_in[:, q_cols + k_cols :],
        sum_out,
        sum_gateup[:, :f_cols],
        sum_gateup[:, f_cols:],
        sum_down,
    )


def solution(mesh):
    return jax.shard_map(
        on_device,
        mesh=mesh,
        in_specs=(
            P(("dp", "row"), "col"),
            P("col"),
            P("col"),
            P("col", "row"),
            P("col", "row"),
            P("col", "row"),
            P("row", "col"),
            P("col", "row"),
            P("col", "row"),
            P("row", "col"),
            P(("dp", "row"), "col"),
        ),
        out_specs=(
            P(("dp", "row"), "col"),
            P(("dp", "row"), "col"),
            P("col"),
            P("col"),
            P("col", "row"),
            P("col", "row"),
            P("col", "row"),
            P("row", "col"),
            P("col", "row"),
            P("col", "row"),
            P("row", "col"),
        ),
        check_vma=False,
    )
```

profile of v0, /device:TPU:0, one launch (start us, length us, event | category | flops | bytes accessed | tf_op | source)
XLA Modules:
  0.0 1411.9 jit_solution(6619210359016683264)
XLA Ops:
  14.7 46.1 %all-gather.5.cloned.1.call-done = bf16[2048,768]{1,0:T(8,128)(2,1)} async-done(((bf16[512,768]{1,0:T(8,128)(2,1)}), bf16[2048,768]{1,0:T(8,128)(2,1)}) %all-gather.5.cloned.1.call-update) | async-done | bytes 3145744 | tf_op jit(solution)/shard_map/all_gather | solution.py:139
  60.9 7.2 fusion.111
  69.6 30.8 %all-reduce.8.cloned.1.call-done = f32[2048,768]{1,0:T(8,128)} async-done(((f32[2048,768]{1,0:T(8,128)}), f32[2048,768]{1,0:T(8,128)}) %all-reduce.8.cloned.1.call-update) | async-done | bytes 6291472 | tf_op jit(solution)/shard_map/psum | solution.py:143
  100.4 3.0 slice.119
  103.5 2.9 copy.41
  106.4 3.8 slice.114
  110.2 3.5 copy.40
  118.5 3.1 convert.47
  126.4 25.8 %while.54 = (s32[]{:T(128)}, bf16[2,512,384]{2,1,0:T(8,128)(2,1)}, f32[2,2,2,512]{3,2,1,0:T(2,128)S(1)}, s32[2]{0:T(128)}, bf16[2,512,2,2,96]{1,4,3,2,0:T(8,128)...) while((s32[]{:T(128)}, bf16[2,512,384]{2,1,0:T(8,128)(2,1)}, ...), condition=%wide.region_6.7_spmd, body=%wide.region_3.6_spmd.sunk | while | flops 830994944 | bytes 30478976 | solution.py:71
  132.8 4.4 fusion.187
  145.7 4.4 fusion.187
  153.0 3.2 reshape.341
  160.8 24.7 %while.55 = (s32[]{:T(128)}, bf16[2,512,384]{2,1,0:T(8,128)(2,1)}, f32[2,2,2,512]{3,2,1,0:T(2,128)}, s32[2]{0:T(128)}, bf16[2,512,2,2,96]{1,4,3,2,0:T(8,128)(2,1...) while((s32[]{:T(128)}, bf16[2,512,384]{2,1,0:T(8,128)(2,1)}, ...), condition=%wide.region_10.11_spmd, body=%wide.region_7.10_spmd.sunk | while | flops 830994944 | bytes 30610104 | solution.py:71
  167.7 3.6 fusion.190
  179.9 3.6 fusion.190
  185.5 6.6 fusion.106
  192.8 70.7 %reduce-scatter.5.cloned.1.call-done = f32[512,768]{1,0:T(8,128)} async-done(((f32[2048,768]{1,0:T(8,128)}), f32[512,768]{1,0:T(8,128)}) %reduce-scatter.5.cloned.1.call-update) | async-done | bytes 1572880 | tf_op jit(solution)/shard_map/reduce_scatter | solution.py:147
  269.0 2.8 constant_dynamic-update-slice_fusion.3
  273.1 36.0 %all-gather.9.cloned.1.call-done = bf16[2048,768]{1,0:T(8,128)(2,1)} async-done(((bf16[512,768]{1,0:T(8,128)(2,1)}), bf16[2048,768]{1,0:T(8,128)(2,1)}) %all-gather.9.cloned.1.call-update) | async-done | bytes 3145744 | tf_op jit(solution)/shard_map/all_gather | solution.py:139
  309.1 7.6 fusion.130
  316.7 38.5 %all-gather.7.cloned.1.call-done = bf16[2048,768]{1,0:T(8,128)(2,1)} async-done(((bf16[512,768]{1,0:T(8,128)(2,1)}), bf16[2048,768]{1,0:T(8,128)(2,1)}) %all-gather.7.cloned.1.call-update) | async-done | bytes 3145744 | tf_op jit(solution)/shard_map/all_gather | solution.py:139
  355.2 12.5 fusion.128
  367.8 82.7 %all-reduce.12.cloned.1.call-done = (f32[2048,2048]{1,0:T(8,128)}, f32[2048,1024]{1,0:T(8,128)}) async-done(((f32[2048,2048]{1,0:T(8,128)}, f32[2048,1024]{1,0:T(8,128)}), (f32[2048,2048]{1,0:T(8,128)}, f32[2048,1024]{1,0:T(8,128)})) %all-reduce.12.cloned.1.call-update) | async-done | bytes 25165840 | tf_op jit(solution)/shard_map/psum | solution.py:143
  450.5 12.9 multiply_convert_fusion.1
  466.6 10.5 fusion.95
  477.1 8.5 fusion.129
  485.7 62.8 %reduce-scatter.9.cloned.1.call-done = f32[512,768]{1,0:T(8,128)} async-done(((f32[2048,768]{1,0:T(8,128)}), f32[512,768]{1,0:T(8,128)}) %reduce-scatter.9.cloned.1.call-update) | async-done | bytes 1572880 | tf_op jit(solution)/shard_map/reduce_scatter | solution.py:147
  553.5 68.1 %reduce-scatter.7.cloned.1.call-done = f32[512,768]{1,0:T(8,128)} async-done(((f32[2048,768]{1,0:T(8,128)}), f32[512,768]{1,0:T(8,128)}) %reduce-scatter.7.cloned.1.call-update) | async-done | bytes 1572880 | tf_op jit(solution)/shard_map/reduce_scatter | solution.py:147
  621.6 4.1 fusion.123
  625.8 43.9 %all-gather.11.cloned.1.call-done = bf16[2048,768]{1,0:T(8,128)(2,1)} async-done(((bf16[512,768]{1,0:T(8,128)(2,1)}), bf16[2048,768]{1,0:T(8,128)(2,1)}) %all-gather.11.cloned.1.call-update) | async-done | bytes 3145744 | tf_op jit(solution)/shard_map/all_gather | solution.py:139
  669.8 5.5 fusion.131
  675.3 12.2 all-reduce.13
  688.8 4.8 reshape.360
  697.6 74.2 %while.56 = (s32[]{:T(128)}, f32[1024,2,96]{0,2,1:T(8,128)}, f32[1024,2,96]{0,2,1:T(8,128)}, f32[2,512,384]{1,0,2:T(2,128)}, bf16[2,512,2,2,96]{1,4,3,2,0:T(8,12...) while((s32[]{:T(128)}, f32[1024,2,96]{0,2,1:T(8,128)}, ...), condition=%wide.region_23.24_spmd.clone, body=%wide.region_21.23_spmd.clone.sunk | while | flops 2046425600 | bytes 131526960 | solution.py:125
  700.6 4.5 fusion.200
  709.8 14.9 %dynamic_update_slice.36 = f32[2,512,384]{1,0,2:T(2,128)} dynamic-update-slice(f32[2,512,384]{1,0,2:T(2,128)} %get-tuple-element.816, f32[1,512,384]{1,0,2:T(1,128)S(1)} %copy.94, s32[]{:T(128)} %get-tuple-element.813, s32[]{:T(128)} %constant.122.clone.1..sunk, s32[]{:T(128)} %constant.122.clone.1..sunk) | dynamic-update-slice | bytes 1572868 | tf_op jit(solution)/shard_map/while/body/jit(dynamic_update_index_in_dim)/dynamic_update_slice | solution.py:71
  724.8 4.0 fusion.202
  728.8 5.7 fusion.203
  737.5 4.5 fusion.200
  746.7 14.9 %dynamic_update_slice.36 = f32[2,512,384]{1,0,2:T(2,128)} dynamic-update-slice(f32[2,512,384]{1,0,2:T(2,128)} %get-tuple-element.816, f32[1,512,384]{1,0,2:T(1,128)S(1)} %copy.94, s32[]{:T(128)} %get-tuple-element.813, s32[]{:T(128)} %constant.122.clone.1..sunk, s32[]{:T(128)} %constant.122.clone.1..sunk) | dynamic-update-slice | bytes 1572868 | tf_op jit(solution)/shard_map/while/body/jit(dynamic_update_index_in_dim)/dynamic_update_slice | solution.py:71
  761.6 4.2 fusion.202
  765.8 5.9 fusion.203
  775.7 4.7 reshape.361
  780.4 3.6 copy.54
  785.5 70.2 %while.57 = (s32[]{:T(128)}, f32[1024,2,96]{0,2,1:T(8,128)S(1)}, f32[1024,2,96]{0,2,1:T(8,128)}, f32[2,512,384]{1,0,2:T(2,128)}, bf16[2,512,2,2,96]{1,4,3,2,0:T(...) while((s32[]{:T(128)}, f32[1024,2,96]{0,2,1:T(8,128)S(1)}, ...), condition=%wide.region_26.27_spmd.clone, body=%wide.region_24.26_spmd.clone.sunk | while | flops 2046425600 | bytes 133099856 | solution.py:125
  788.7 3.2 fusion.213
  796.6 14.9 %dynamic_update_slice.37 = f32[2,512,384]{1,0,2:T(2,128)} dynamic-update-slice(f32[2,512,384]{1,0,2:T(2,128)} %get-tuple-element.777, f32[1,512,384]{1,0,2:T(1,128)S(1)} %copy.95, s32[]{:T(128)} %get-tuple-element.774, s32[]{:T(128)} %constant.122.clone.1..sunk.1, s32[]{:T(128)} %constant.122.clone.1..sunk.1) | dynamic-update-slice | bytes 1572868 | tf_op jit(solution)/shard_map/while/body/jit(dynamic_update_index_in_dim)/dynamic_update_slice | solution.py:71
  811.5 3.2 fusion.215
  814.7 5.8 fusion.216
  823.7 3.2 fusion.213
  831.6 14.9 %dynamic_update_slice.37 = f32[2,512,384]{1,0,2:T(2,128)} dynamic-update-slice(f32[2,512,384]{1,0,2:T(2,128)} %get-tuple-element.777, f32[1,512,384]{1,0,2:T(1,128)S(1)} %copy.95, s32[]{:T(128)} %get-tuple-element.774, s32[]{:T(128)} %constant.122.clone.1..sunk.1, s32[]{:T(128)} %constant.122.clone.1..sunk.1) | dynamic-update-slice | bytes 1572868 | tf_op jit(solution)/shard_map/while/body/jit(dynamic_update_index_in_dim)/dynamic_update_slice | solution.py:71
  846.5 3.2 fusion.215
  849.7 6.0 fusion.216
  855.8 3.7 concatenate.55
  868.3 5.5 fusion.109
  873.9 8.5 fusion.132
  882.4 9.1 fusion.94
  894.5 4.1 fusion.108
  898.7 45.4 %reduce-scatter.11.cloned.1.call-done = f32[512,768]{1,0:T(8,128)} async-done(((f32[2048,768]{1,0:T(8,128)}), f32[512,768]{1,0:T(8,128)}) %reduce-scatter.11.cloned.1.call-update) | async-done | bytes 1572880 | tf_op jit(solution)/shard_map/reduce_scatter | solution.py:147
  948.6 44.6 %all-reduce = (f32[768]{0:T(1024)}, f32[768]{0:T(1024)}) all-reduce(f32[768]{0:T(1024)S(1)} %get-tuple-element.363, f32[768]{0:T(1024)S(1)} %copy-done.59), channel_id=1, replica_groups=mesh['dp'=4,'row'=4,'col'=2] {'dp','row'}, use_global_device_ids=true, to_apply=%region_31.32 | all-reduce | flops 1536 | bytes 12288 | tf_op jit(solution)/shard_map/psum | solution.py:228
  993.2 3.0 fusion.101
  996.3 391.9 %all-reduce.10.cloned.1.call-done = (f32[768,768]{1,0:T(8,128)}, f32[384,768]{1,0:T(8,128)}, f32[768,2048]{1,0:T(8,128)}, f32[1024,768]{1,0:T(8,128)}) async-done(((f32[768,768]{1,0:T(8,128)}, f32[384,768]{1,0:T(8,128)}, f32[768,2048]{1,0:T(8,128)}, f32[1024,768]{1,0:T(8,128)}), (f32[768,768]{1,0:T(8,128)}, f32[384,768]{1,0:T(8,128)}, f32[768,2048]{1,0:T(8,128)}, ...) | async-done | bytes 12976144 | tf_op jit(solution)/shard_map/psum | solution.py:222
  1391.4 6.7 fusion.124
  1401.2 3.8 copy.157
  (301 shorter events, 132.7 us)
Async XLA Ops:
  7.2 301.9 %copy-start = (bf16[1024,768]{1,0:T(8,128)(2,1)S(1)}, bf16[1024,768]{1,0:T(8,128)(2,1)}, u32[]{:S(2)}) copy-start(bf16[1024,768]{1,0:T(8,128)(2,1)} %param.28) | copy-start | bytes 4718596
  7.2 7.2 copy-start.48
  7.2 7.3 copy-start.49
  7.2 53.6 %copy-start.64 = (bf16[768,384]{1,0:T(8,128)(2,1)S(1)}, bf16[768,384]{1,0:T(8,128)(2,1)}, u32[]{:S(2)}) copy-start(bf16[768,384]{1,0:T(8,128)(2,1)} %param.22) | copy-start | bytes 1769476
  7.2 53.6 %all-gather.5.cloned.1.call-start = ((), (), s32[]{:S(2)}) async-start(), calls=%async_computation.4 | async-start | bytes 3932160 | tf_op jit(solution)/shard_map/all_gather | solution.py:139
  14.3 86.1 %all-reduce.8.cloned.1.call-start = ((), (), s32[]{:S(2)}) async-start(), calls=%async_computation.5 | async-start | bytes 12582912 | tf_op jit(solution)/shard_map/psum | solution.py:143
  14.5 53.5 %copy-start.42 = (bf16[768,192]{1,0:T(8,128)(2,1)}, bf16[768,192]{1,0:T(8,128)(2,1)S(1)}, u32[]{:S(2)}) copy-start(bf16[768,192]{1,0:T(8,128)(2,1)S(1)} %copy.38) | copy-start | bytes 884740
  14.7 53.4 %copy-start.44 = (bf16[768,192]{1,0:T(8,128)(2,1)}, bf16[768,192]{1,0:T(8,128)(2,1)S(1)}, u32[]{:S(2)}) copy-start(bf16[768,192]{1,0:T(8,128)(2,1)S(1)} %copy.39) | copy-start | bytes 884740
  68.1 195.4 %reduce-scatter.5.cloned.1.call-start = ((), (), s32[]{:S(2)}) async-start(), calls=%async_computation.6 | async-start | bytes 7864320 | tf_op jit(solution)/shard_map/reduce_scatter | solution.py:147
  69.6 46.7 %copy-start.20 = (f32[2048,48]{0,1:T(8,128)}, f32[2048,48]{0,1:T(8,128)S(1)}, u32[]{:S(2)}) copy-start(f32[2048,48]{0,1:T(8,128)S(1)} %get-tuple-element.477) | copy-start | bytes 1179652
  69.6 46.7 %copy-start.22 = (f32[2048,48]{0,1:T(8,128)}, f32[2048,48]{0,1:T(8,128)S(1)}, u32[]{:S(2)}) copy-start(f32[2048,48]{0,1:T(8,128)S(1)} %get-tuple-element.478) | copy-start | bytes 1179652
  152.1 8.7 copy-start.8
  152.1 8.7 copy-start.50
  167.7 3.7 copy-start.53
  179.8 3.7 copy-start.53
  185.5 6.6 copy-start.6
  185.5 6.6 copy-start.10
  185.5 6.6 copy-start.16
  192.1 75.7 %copy-start.55 = (f32[768]{0:T(1024)S(1)}, f32[768]{0:T(1024)}, u32[]{:S(2)}) copy-start(f32[768]{0:T(1024)} %param.21) | copy-start | bytes 9220
  192.1 116.9 %all-gather.9.cloned.1.call-start = ((), (), s32[]{:S(2)}) async-start(), calls=%async_computation.9 | async-start | bytes 3932160 | tf_op jit(solution)/shard_map/all_gather | solution.py:139
  192.7 162.5 %all-gather.7.cloned.1.call-start = ((), (), s32[]{:S(2)}) async-start(), calls=%async_computation.7 | async-start | bytes 3932160 | tf_op jit(solution)/shard_map/all_gather | solution.py:139
  269.0 181.5 %all-reduce.12.cloned.1.call-start = ((), (), s32[]{:S(2)}) async-start(), calls=%async_computation.14 | async-start | bytes 50331648 | tf_op jit(solution)/shard_map/psum | solution.py:143
  367.7 180.8 %reduce-scatter.9.cloned.1.call-start = ((), (), s32[]{:S(2)}) async-start(), calls=%async_computation.10 | async-start | bytes 7864320 | tf_op jit(solution)/shard_map/reduce_scatter | solution.py:147
  463.4 3.2 copy-start.32
  477.1 144.5 %reduce-scatter.7.cloned.1.call-start = ((), (), s32[]{:S(2)}) async-start(), calls=%async_computation.8 | async-start | bytes 7864320 | tf_op jit(solution)/shard_map/reduce_scatter | solution.py:147
  485.6 184.1 %all-gather.11.cloned.1.call-start = ((), (), s32[]{:S(2)}) async-start(), calls=%async_computation.11 | async-start | bytes 3932160 | tf_op jit(solution)/shard_map/all_gather | solution.py:139
  548.5 73.1 %copy-start.29 = (f32[512,768]{1,0:T(8,128)S(1)}, f32[512,768]{1,0:T(8,128)}, u32[]{:S(2)}) copy-start(f32[512,768]{1,0:T(8,128)} %reduce-scatter.9.cloned.1.call-done) | copy-start | bytes 4718596
  625.8 318.3 %reduce-scatter.11.cloned.1.call-start = ((), (), s32[]{:S(2)}) async-start(), calls=%async_computation.12 | async-start | bytes 7864320 | tf_op jit(solution)/shard_map/reduce_scatter | solution.py:147
  688.8 8.8 copy-start.9
  688.8 8.8 copy-start.13
  688.8 8.8 copy-start.51
  698.9 6.2 copy-start.2
  724.8 4.0 copy-start.27
  735.8 6.2 copy-start.2
  761.6 4.2 copy-start.27
  775.7 9.8 copy-start.7
  775.7 9.8 copy-start.11
  775.7 9.8 copy-start.17
  775.7 9.8 copy-start.54
  785.6 3.1 copy-start.24
  786.9 5.0 copy-start.3
  811.5 3.2 copy-start.25
  814.7 5.8 copy-start.18
  820.5 3.1 copy-start.24
  821.9 5.1 copy-start.3
  846.5 3.2 copy-start.25
  849.7 6.1 copy-start.18
  855.8 6.4 copy-start.21
  855.8 6.4 copy-start.23
  867.8 6.0 copy-start.40
  873.8 514.3 %all-reduce.10.cloned.1.call-start = ((), (), s32[]{:S(2)}) async-start(), calls=%async_computation.13 | async-start | bytes 25952256 | tf_op jit(solution)/shard_map/psum | solution.py:222
  873.9 8.5 copy-start.31
  873.9 8.5 copy-start.33
  873.9 8.5 copy-start.62
  882.4 9.1 copy-start.35
  882.4 9.1 copy-start.36
  882.4 9.1 copy-start.63
  898.6 45.4 %copy-start.15 = (bf16[512,768]{1,0:T(8,128)(2,1)S(1)}, bf16[512,768]{1,0:T(8,128)(2,1)}, u32[]{:S(2)}) copy-start(bf16[512,768]{1,0:T(8,128)(2,1)} %param.19) | copy-start | bytes 2359300
  898.6 45.4 %copy-start.56 = (f32[768]{0:T(1024)S(1)}, f32[768]{0:T(1024)}, u32[]{:S(2)}) copy-start(f32[768]{0:T(1024)} %param.20) | copy-start | bytes 9220
  898.6 45.4 %copy-start.58 = (f32[512]{0:T(512)S(1)}, f32[512]{0:T(512)}, u32[]{:S(2)}) copy-start(f32[512]{0:T(512)} %copy-done.57) | copy-start | bytes 6148
  898.6 50.0 %copy-start.59 = (f32[768]{0:T(1024)S(1)}, f32[768]{0:T(1024)}, u32[]{:S(2)}) copy-start(f32[768]{0:T(1024)} %get-tuple-element.361) | copy-start | bytes 9220
  898.6 94.6 %copy-start.60 = (f32[512]{0:T(512)S(1)}, f32[512]{0:T(512)}, u32[]{:S(2)}) copy-start(f32[512]{0:T(512)} %get-tuple-element.479) | copy-start | bytes 6148
  944.1 49.2 %copy-start.28 = (f32[512,768]{1,0:T(8,128)S(1)}, f32[512,768]{1,0:T(8,128)}, u32[]{:S(2)}) copy-start(f32[512,768]{1,0:T(8,128)} %reduce-scatter.11.cloned.1.call-done) | copy-start | bytes 4718596
  1400.2 4.8 copy-start.1
  (24 other events, 54.2 us)
Sparse Core Ops, SparseCore 0:
  14.4 46.4 all-gather.4
  68.2 32.1 all-reduce.7
  192.2 71.2 reduce-scatter.4
  265.2 43.8 all-gather.8
  311.3 43.8 all-gather.6
  367.8 82.5 all-reduce.11
  477.2 71.2 reduce-scatter.8
  551.5 70.0 reduce-scatter.6
  625.9 43.8 all-gather.10
  874.0 70.0 reduce-scatter.10
  948.1 440.0 all-reduce.9
where the time goes:
time: 1420 us; the launch traced here: 1410 us
  waiting for transfers between devices  918 us (65%)
  matrix products  176 us (12%)
  local copies, waits for them, and re-layouts  161 us (11%)
  other arithmetic  69.4 us (5%)
  blocking collectives  66.8 us (5%)
  between operations  14.9 us (1%)
    psum x1, waiting for transfers between devices, on_device(): lax.psum((gw_down, gw_gateup, gw_in, gw_out), 'dp')  392 us
    reduce_scatter x4, waiting for transfers between devices, token_sum(): lax.psum_scatter(jnp.einsum('tj,jc->tc', source, weight, preferred_elemen...  247 us
    all_gather x4, waiting for transfers between devices, gather_tokens(): return lax.all_gather(values, 'row', axis=0, tiled=True)  165 us
    psum x2, waiting for transfers between devices, width_sum(): return lax.psum(values, 'col')  114 us
    dynamic_update_slice x16, local copies, waits for them, and re-layouts, attend_forward(): mixed, logsum = lax.map(one_block, (query_seq, jnp.arange(count)))  70.9 us
    psum x1, blocking collectives, on_device(): gain_a, gain_f = lax.psum((part_gain_attn, part_gain_ffn), ('dp', 'row'))  44.6 us
    dot_general x4, matrix products, token_sum(): jnp.einsum('tj,jc->tc', source, weight, preferred_element_type=jnp.float32)  31.1 us
  transfers between devices with their start and end apart: 11, of which 11 were waited for; matrix products, arithmetic and copies ran while one was open for 4% of the time, Pallas kernels for 0%

commit v1 on v0

--- a/solution.py
+++ b/solution.py
@@ -8,6 +8,31 @@
 LENGTH = 1024
 EPS = 1e-05
 THETA = 100000.0
+
+
+def units_refer(slab_in):
+    n = jax.lax.axis_size("row")
+    block_list = []
+    at = 0
+    while at < n:
+        block_list.append((at, (at + 1) % n))
+        at = at + 1
+    store = []
+    at = 0
+    while at < n:
+        store.append((at, (at - 1) % n))
+        at = at + 1
+    front, base_arr = ([slab_in], [slab_in])
+    for _ in range(n // 2):
+        front.append(jax.lax.ppermute(front[-1], "row", block_list))
+    dev_i = 0
+    while dev_i < (n - 1) // 2:
+        t1 = jax.lax.ppermute(base_arr[-1], "row", store)
+        base_arr.append(t1)
+        dev_i += 1
+    inter = jnp.concatenate([*front[::-1], *base_arr[1:]], 0)
+    work_now = jnp.roll(inter, (jax.lax.axis_index("row") - n // 2) * slab_in.shape[0], 0)
+    return work_now
 
 
 def rotate(values, heads, inverse):
@@ -136,7 +161,7 @@
 
 
 def gather_tokens(values):
-    return lax.all_gather(values, "row", axis=0, tiled=True)
+    return units_refer(values)
 
 
 def width_sum(values):

time: 1420 us -> 1520 us (1.070)
  other arithmetic: 69.4 us -> 147 us
  starting transfers between devices: 0.45 us -> 17.1 us
    all_gather x4 -> x0, waiting for transfers between devices: 165 us -> none  [gather_tokens(): return lax.all_gather(values, 'row', axis=0, tiled=True)]
    ppermute x0 -> x12, waiting for transfers between devices: none -> 157 us  [the longest x8 111 us: units_refer(): front.append(jax.lax.ppermute(front[-1], 'row', block_list))]
    concatenate x0 -> x4, other arithmetic: none -> 79.4 us  [units_refer(): jnp.roll(inter, (jax.lax.axis_index('row') - n // 2) * slab_in.shape[0], 0)]
    ppermute x0 -> x12, starting transfers between devices: none -> 16.8 us  [the longest x8 10.5 us: units_refer(): front.append(jax.lax.ppermute(front[-1], 'row', block_list))]
  transfers between devices with their start and end apart: 11 -> 19, of which waited for: 11 -> 17; matrix products, arithmetic and copies ran while one was open for 4% -> 5% of each run, Pallas kernels for 0% -> 0%
where the time goes in v1:
time: 1520 us; the launch traced here: 1500 us
  waiting for transfers between devices  920 us (61%)
  local copies, waits for them, and re-layouts  165 us (11%)
  matrix products  165 us (11%)
  other arithmetic  147 us (10%)
  blocking collectives  66.9 us (4%)
  starting transfers between devices  17.1 us (1%)
    psum x1, waiting for transfers between devices, on_device(): lax.psum((gw_down, gw_gateup, gw_in, gw_out), 'dp')  392 us
    reduce_scatter x4, waiting for transfers between devices, token_sum(): lax.psum_scatter(jnp.einsum('tj,jc->tc', source, weight, preferred_elemen...  257 us
    psum x2, waiting for transfers between devices, width_sum(): return lax.psum(values, 'col')  114 us
    ppermute x8, waiting for transfers between devices, units_refer(): front.append(jax.lax.ppermute(front[-1], 'row', block_list))  111 us
    concatenate x4, other arithmetic, units_refer(): jnp.roll(inter, (jax.lax.axis_index('row') - n // 2) * slab_in.shape[0], 0)  79.4 us
    dynamic_update_slice x16, local copies, waits for them, and re-layouts, attend_forward(): mixed, logsum = lax.map(one_block, (query_seq, jnp.arange(count)))  70.8 us
    ppermute x4, waiting for transfers between devices, units_refer(): t1 = jax.lax.ppermute(base_arr[-1], 'row', store)  45.8 us
    psum x1, blocking collectives, on_device(): gain_a, gain_f = lax.psum((part_gain_attn, part_gain_ffn), ('dp', 'row'))  44.7 us
  transfers between devices with their start and end apart: 19, of which 17 were waited for; matrix products, arithmetic and copies ran while one was open for 5% of the time, Pallas kernels for 0%

profile of v1, /device:TPU:0, one launch (start us, length us, event | category | flops | bytes accessed | tf_op | source)
XLA Modules:
  0.0 1502.7 jit_solution(7602956636046206462)
XLA Ops:
  17.2 18.3 %collective-permute-done = bf16[512,768]{1,0:T(8,128)(2,1)S(1)} collective-permute-done((bf16[512,768]{1,0:T(8,128)(2,1)S(1)}, bf16[512,768]{1,0:T(8,128)(2,1)S(1)}, u32[]{:S(2)}, u32[]{:S(2)}) %collective-permute-start) | collective-permute-done | bytes 786464 | tf_op jit(solution)/shard_map/ppermute | solution.py:27
  39.8 13.2 collective-permute-done.2
  53.0 15.8 %collective-permute-done.1 = bf16[512,768]{1,0:T(8,128)(2,1)} collective-permute-done((bf16[512,768]{1,0:T(8,128)(2,1)S(1)}, bf16[512,768]{1,0:T(8,128)(2,1)}, u32[]{:S(2)}, u32[]{:S(2)}) %collective-permute-start.1) | collective-permute-done | bytes 786464 | tf_op jit(solution)/shard_map/ppermute | solution.py:27
  68.8 15.6 %fusion.120 = bf16[2048,768]{1,0:T(8,128)(2,1)S(1)} fusion(s32[]{:T(128)S(6)} %select_n.93, bf16[512,768]{1,0:T(8,128)(2,1)} %collective-permute-done.1, bf16[512,768]{1,0:T(8,128)(2,1)S(1)} %collective-permute-done, bf16[512,768]{1,0:T(8,128)(2,1)S(1)} %fusion.126, bf16[512,768]{1,0:T(8,128)(2,1)} %collective-permute-done.2), kind=kLoop, calls=%fused_computation.185 | loop fusion | flops 25165824 | bytes 6291460 | tf_op jit(solution)/shard_map/jit(_roll_dynamic)/concatenate | solution.py:34
  86.1 4.8 fusion.139
  92.4 31.3 %all-reduce.8.cloned.1.call-done = f32[2048,768]{1,0:T(8,128)} async-done(((f32[2048,768]{1,0:T(8,128)}), f32[2048,768]{1,0:T(8,128)}) %all-reduce.8.cloned.1.call-update) | async-done | bytes 6291472 | tf_op jit(solution)/shard_map/psum | solution.py:168
  129.8 3.8 slice.114
  133.5 3.5 copy.40
  149.7 25.8 %while.54 = (s32[]{:T(128)}, bf16[2,512,384]{2,1,0:T(8,128)(2,1)}, f32[2,2,2,512]{3,2,1,0:T(2,128)S(1)}, s32[2]{0:T(128)}, bf16[2,512,2,2,96]{1,4,3,2,0:T(8,128)...) while((s32[]{:T(128)}, bf16[2,512,384]{2,1,0:T(8,128)(2,1)}, ...), condition=%wide.region_6.8_spmd, body=%wide.region_3.7_spmd.sunk | while | flops 830994944 | bytes 30478976 | solution.py:96
  156.2 4.4 fusion.215
  169.1 4.4 fusion.215
  184.2 24.7 %while.55 = (s32[]{:T(128)}, bf16[2,512,384]{2,1,0:T(8,128)(2,1)}, f32[2,2,2,512]{3,2,1,0:T(2,128)}, s32[2]{0:T(128)}, bf16[2,512,2,2,96]{1,4,3,2,0:T(8,128)(2,1...) while((s32[]{:T(128)}, bf16[2,512,384]{2,1,0:T(8,128)(2,1)}, ...), condition=%wide.region_10.12_spmd, body=%wide.region_7.11_spmd.sunk | while | flops 830994944 | bytes 30610104 | solution.py:96
  191.1 3.6 fusion.218
  203.3 3.6 fusion.218
  208.9 6.6 fusion.134
  217.4 80.9 %reduce-scatter.5.cloned.1.call-done = f32[512,768]{1,0:T(8,128)} async-done(((f32[2048,768]{1,0:T(8,128)}), f32[512,768]{1,0:T(8,128)}) %reduce-scatter.5.cloned.1.call-update) | async-done | bytes 1572880 | tf_op jit(solution)/shard_map/reduce_scatter | solution.py:172
  309.1 15.1 %collective-permute-done.3 = bf16[512,768]{1,0:T(8,128)(2,1)S(1)} collective-permute-done((bf16[512,768]{1,0:T(8,128)(2,1)S(1)}, bf16[512,768]{1,0:T(8,128)(2,1)S(1)}, u32[]{:S(2)}, u32[]{:S(2)}) %collective-permute-start.3) | collective-permute-done | bytes 786464 | tf_op jit(solution)/shard_map/ppermute | solution.py:27
  324.8 16.3 %collective-permute-done.8 = bf16[512,768]{1,0:T(8,128)(2,1)S(1)} collective-permute-done((bf16[512,768]{1,0:T(8,128)(2,1)}, bf16[512,768]{1,0:T(8,128)(2,1)S(1)}, u32[]{:S(2)}, u32[]{:S(2)}) %collective-permute-start.8) | collective-permute-done | bytes 786464 | tf_op jit(solution)/shard_map/ppermute | solution.py:30
  341.1 16.8 %collective-permute-done.7 = bf16[512,768]{1,0:T(8,128)(2,1)S(1)} collective-permute-done((bf16[512,768]{1,0:T(8,128)(2,1)}, bf16[512,768]{1,0:T(8,128)(2,1)S(1)}, u32[]{:S(2)}, u32[]{:S(2)}) %collective-permute-start.7) | collective-permute-done | bytes 786464 | tf_op jit(solution)/shard_map/ppermute | solution.py:27
  357.9 16.0 %fusion.106 = bf16[2048,768]{1,0:T(8,128)(2,1)S(1)} fusion(s32[]{:T(128)S(6)} %select_n.93, bf16[512,768]{1,0:T(8,128)(2,1)S(1)} %collective-permute-done.7, bf16[512,768]{1,0:T(8,128)(2,1)} %collective-permute-done.6, bf16[512,768]{1,0:T(8,128)(2,1)} %param.31, bf16[512,768]{1,0:T(8,128)(2,1)S(1)} %collective-permute-done.8), kind=kLoop, calls=%fused_computation.171 | loop fusion | flops 25165824 | bytes 6291460 | tf_op jit(solution)/shard_map/jit(_roll_dynamic)/concatenate | solution.py:34
  374.0 5.9 fusion.158
  379.9 10.9 collective-permute-done.4
  390.8 28.9 %fusion.113 = bf16[2048,768]{1,0:T(8,128)(2,1)S(1)} fusion(s32[]{:T(128)S(6)} %select_n.93, bf16[512,768]{1,0:T(8,128)(2,1)S(1)} %collective-permute-done.4, bf16[512,768]{1,0:T(8,128)(2,1)S(1)} %collective-permute-done.3, bf16[512,768]{1,0:T(8,128)(2,1)S(1)} %multiply_convert_fusion.3, bf16[512,768]{1,0:T(8,128)(2,1)S(1)} %collective-permute-done.5), kind=kLoop, calls=%fused_computation.178 | loop fusion | flops 25165824 | bytes 6291460 | tf_op jit(solution)/shard_map/jit(_roll_dynamic)/concatenate | solution.py:34
  421.5 9.5 fusion.156
  431.1 82.7 %all-reduce.12.cloned.1.call-done = (f32[2048,2048]{1,0:T(8,128)}, f32[2048,1024]{1,0:T(8,128)}) async-done(((f32[2048,2048]{1,0:T(8,128)}, f32[2048,1024]{1,0:T(8,128)}), (f32[2048,2048]{1,0:T(8,128)}, f32[2048,1024]{1,0:T(8,128)})) %all-reduce.12.cloned.1.call-update) | async-done | bytes 25165840 | tf_op jit(solution)/shard_map/psum | solution.py:168
  513.8 13.3 multiply_convert_fusion.1
  530.3 8.6 fusion.95
  539.0 8.5 fusion.157
  547.6 62.8 %reduce-scatter.9.cloned.1.call-done = f32[512,768]{1,0:T(8,128)} async-done(((f32[2048,768]{1,0:T(8,128)}), f32[512,768]{1,0:T(8,128)}) %reduce-scatter.9.cloned.1.call-update) | async-done | bytes 1572880 | tf_op jit(solution)/shard_map/reduce_scatter | solution.py:172
  615.4 67.9 %reduce-scatter.7.cloned.1.call-done = f32[512,768]{1,0:T(8,128)} async-done(((f32[2048,768]{1,0:T(8,128)}), f32[512,768]{1,0:T(8,128)}) %reduce-scatter.7.cloned.1.call-update) | async-done | bytes 1572880 | tf_op jit(solution)/shard_map/reduce_scatter | solution.py:172
  683.3 4.1 fusion.151
  690.4 18.6 %collective-permute-done.9 = bf16[512,768]{1,0:T(8,128)(2,1)S(1)} collective-permute-done((bf16[512,768]{1,0:T(8,128)(2,1)}, bf16[512,768]{1,0:T(8,128)(2,1)S(1)}, u32[]{:S(2)}, u32[]{:S(2)}) %collective-permute-start.9) | collective-permute-done | bytes 786464 | tf_op jit(solution)/shard_map/ppermute | solution.py:27
  709.6 16.3 %collective-permute-done.11 = bf16[512,768]{1,0:T(8,128)(2,1)S(1)} collective-permute-done((bf16[512,768]{1,0:T(8,128)(2,1)}, bf16[512,768]{1,0:T(8,128)(2,1)S(1)}, u32[]{:S(2)}, u32[]{:S(2)}) %collective-permute-start.11) | collective-permute-done | bytes 786464 | tf_op jit(solution)/shard_map/ppermute | solution.py:30
  725.8 15.6 %collective-permute-done.10 = bf16[512,768]{1,0:T(8,128)(2,1)S(1)} collective-permute-done((bf16[512,768]{1,0:T(8,128)(2,1)S(1)}, bf16[512,768]{1,0:T(8,128)(2,1)S(1)}, u32[]{:S(2)}, u32[]{:S(2)}) %collective-permute-start.10) | collective-permute-done | bytes 786464 | tf_op jit(solution)/shard_map/ppermute | solution.py:27
  741.4 18.8 %fusion.99 = bf16[2048,768]{1,0:T(8,128)(2,1)S(1)} fusion(s32[]{:T(128)S(6)} %select_n.93, bf16[512,768]{1,0:T(8,128)(2,1)S(1)} %collective-permute-done.10, bf16[512,768]{1,0:T(8,128)(2,1)S(1)} %collective-permute-done.9, bf16[512,768]{1,0:T(8,128)(2,1)} %get-tuple-element.442, bf16[512,768]{1,0:T(8,128)(2,1)S(1)} %collective-permute-done.11), kind=kLoop, calls=%fused_computation.164 | loop fusion | flops 25165824 | bytes 6291460 | tf_op jit(solution)/shard_map/jit(_roll_dynamic)/concatenate | solution.py:34
  761.9 3.5 fusion.159
  765.4 12.2 all-reduce.13
  778.9 4.8 reshape.360
  787.7 74.6 %while.56 = (s32[]{:T(128)}, f32[1024,2,96]{0,2,1:T(8,128)}, f32[1024,2,96]{0,2,1:T(8,128)}, f32[2,512,384]{1,0,2:T(2,128)}, bf16[2,512,2,2,96]{1,4,3,2,0:T(8,12...) while((s32[]{:T(128)}, f32[1024,2,96]{0,2,1:T(8,128)}, ...), condition=%wide.region_23.25_spmd.clone, body=%wide.region_21.24_spmd.clone.sunk | while | flops 2046425600 | bytes 131526960 | solution.py:150
  791.0 4.5 fusion.228
  800.2 14.9 dynamic_update_slice.36
  815.1 4.0 fusion.230
  819.1 5.7 fusion.231
  828.0 4.5 fusion.228
  837.3 14.9 dynamic_update_slice.36
  852.2 4.2 fusion.230
  856.4 6.0 fusion.231
  866.3 4.7 reshape.361
  871.0 3.6 copy.54
  876.2 70.0 %while.57 = (s32[]{:T(128)}, f32[1024,2,96]{0,2,1:T(8,128)S(1)}, f32[1024,2,96]{0,2,1:T(8,128)}, f32[2,512,384]{1,0,2:T(2,128)}, bf16[2,512,2,2,96]{1,4,3,2,0:T(...) while((s32[]{:T(128)}, f32[1024,2,96]{0,2,1:T(8,128)S(1)}, ...), condition=%wide.region_26.28_spmd.clone, body=%wide.region_24.27_spmd.clone.sunk | while | flops 2046425600 | bytes 133099856 | solution.py:150
  887.2 14.9 dynamic_update_slice.37
  905.3 5.8 fusion.244
  922.1 14.9 dynamic_update_slice.37
  940.2 6.0 fusion.244
  946.2 3.7 concatenate.74
  958.7 5.5 fusion.137
  964.3 8.5 fusion.160
  972.9 9.1 fusion.94
  984.9 4.1 fusion.136
  989.0 45.4 %reduce-scatter.11.cloned.1.call-done = f32[512,768]{1,0:T(8,128)} async-done(((f32[2048,768]{1,0:T(8,128)}), f32[512,768]{1,0:T(8,128)}) %reduce-scatter.11.cloned.1.call-update) | async-done | bytes 1572880 | tf_op jit(solution)/shard_map/reduce_scatter | solution.py:172
  1039.1 44.7 %all-reduce = (f32[768]{0:T(1024)}, f32[768]{0:T(1024)}) all-reduce(f32[768]{0:T(1024)S(1)} %get-tuple-element.364, f32[768]{0:T(1024)S(1)} %copy-done.68), channel_id=1, replica_groups=mesh['dp'=4,'row'=4,'col'=2] {'dp','row'}, use_global_device_ids=true, to_apply=%region_31.33 | all-reduce | flops 1536 | bytes 12288 | tf_op jit(solution)/shard_map/psum | solution.py:253
  1086.7 391.8 %all-reduce.10.cloned.1.call-done = (f32[768,768]{1,0:T(8,128)}, f32[384,768]{1,0:T(8,128)}, f32[768,2048]{1,0:T(8,128)}, f32[1024,768]{1,0:T(8,128)}) async-done(((f32[768,768]{1,0:T(8,128)}, f32[384,768]{1,0:T(8,128)}, f32[768,2048]{1,0:T(8,128)}, f32[1024,768]{1,0:T(8,128)}), (f32[768,768]{1,0:T(8,128)}, f32[384,768]{1,0:T(8,128)}, f32[768,2048]{1,0:T(8,128)}, ...) | async-done | bytes 12976144 | tf_op jit(solution)/shard_map/psum | solution.py:247
  1481.8 6.7 fusion.152
  1491.7 3.8 copy.157
  (329 shorter events, 182.2 us)
Async XLA Ops:
  7.2 366.8 %copy-start = (bf16[1024,768]{1,0:T(8,128)(2,1)S(1)}, bf16[1024,768]{1,0:T(8,128)(2,1)}, u32[]{:S(2)}) copy-start(bf16[1024,768]{1,0:T(8,128)(2,1)} %param.30) | copy-start | bytes 4718596
  7.2 116.6 %all-reduce.8.cloned.1.call-start = ((), (), s32[]{:S(2)}) async-start(), calls=%async_computation.4 | async-start | bytes 12582912 | tf_op jit(solution)/shard_map/psum | solution.py:168
  11.9 23.6 %copy-start.66 = (f32[512]{0:T(512)}, f32[512]{0:T(512)S(1)}, u32[]{:S(2)}) copy-start(f32[512]{0:T(512)S(1)} %get-tuple-element.481) | copy-start | bytes 6148
  13.3 22.2 %collective-permute-start = (bf16[512,768]{1,0:T(8,128)(2,1)S(1)}, bf16[512,768]{1,0:T(8,128)(2,1)S(1)}, u32[]{:S(2)}, u32[]{:S(2)}) collective-permute-start(bf16[512,768]{1,0:T(8,128)(2,1)S(1)} %fusion.126), channel_id=1, source_target_pairs={{0,2},{2,4},{4,6},{6,0},{1,3},{3,5},{5,7},{7,1},{8,10},{10,12},{12... | collective-permute-start | bytes 2359304 | tf_op jit(solution)/shard_map/ppermute | solution.py:27
  16.2 36.8 %collective-permute-start.2 = (bf16[512,768]{1,0:T(8,128)(2,1)S(1)}, bf16[512,768]{1,0:T(8,128)(2,1)}, u32[]{:S(2)}, u32[]{:S(2)}) collective-permute-start(bf16[512,768]{1,0:T(8,128)(2,1)S(1)} %fusion.126), channel_id=1, source_target_pairs={{0,6},{2,0},{4,2},{6,4},{1,7},{3,1},{5,3},{7,5},{8,14},{10,8},{12,... | collective-permute-start | bytes 2359304 | tf_op jit(solution)/shard_map/ppermute | solution.py:30
  35.5 33.3 %collective-permute-start.1 = (bf16[512,768]{1,0:T(8,128)(2,1)S(1)}, bf16[512,768]{1,0:T(8,128)(2,1)}, u32[]{:S(2)}, u32[]{:S(2)}) collective-permute-start(bf16[512,768]{1,0:T(8,128)(2,1)S(1)} %collective-permute-done), channel_id=1, source_target_pairs={{0,2},{2,4},{4,6},{6,0},{1,3},{3,5},{5,7},{7,1},{8,10},{10,12},{12... | collective-permute-start | bytes 2359304 | tf_op jit(solution)/shard_map/ppermute | solution.py:27
  37.7 46.7 %copy-start.53 = (bf16[768,192]{1,0:T(8,128)(2,1)}, bf16[768,192]{1,0:T(8,128)(2,1)S(1)}, u32[]{:S(2)}) copy-start(bf16[768,192]{1,0:T(8,128)(2,1)S(1)} %copy.38) | copy-start | bytes 884740
  39.8 46.3 %copy-start.55 = (bf16[768,192]{1,0:T(8,128)(2,1)S(1)}, bf16[768,192]{1,0:T(8,128)(2,1)}, u32[]{:S(2)}) copy-start(bf16[768,192]{1,0:T(8,128)(2,1)} %copy.39) | copy-start | bytes 884740
  39.8 46.3 %copy-start.70 = (bf16[768,384]{1,0:T(8,128)(2,1)S(1)}, bf16[768,384]{1,0:T(8,128)(2,1)}, u32[]{:S(2)}) copy-start(bf16[768,384]{1,0:T(8,128)(2,1)} %param.24) | copy-start | bytes 1769476
  90.9 207.4 %reduce-scatter.5.cloned.1.call-start = ((), (), s32[]{:S(2)}) async-start(), calls=%async_computation.5 | async-start | bytes 7864320 | tf_op jit(solution)/shard_map/reduce_scatter | solution.py:172
  92.4 47.3 %copy-start.20 = (f32[2048,48]{0,1:T(8,128)}, f32[2048,48]{0,1:T(8,128)S(1)}, u32[]{:S(2)}) copy-start(f32[2048,48]{0,1:T(8,128)S(1)} %get-tuple-element.478) | copy-start | bytes 1179652
  92.4 47.3 %copy-start.22 = (f32[2048,48]{0,1:T(8,128)}, f32[2048,48]{0,1:T(8,128)S(1)}, u32[]{:S(2)}) copy-start(f32[2048,48]{0,1:T(8,128)S(1)} %get-tuple-element.479) | copy-start | bytes 1179652
  175.5 8.7 copy-start.8
  175.5 8.7 copy-start.59
  208.9 6.6 copy-start.6
  208.9 6.6 copy-start.10
  208.9 6.6 copy-start.16
  215.5 87.1 %copy-start.64 = (f32[768]{0:T(1024)S(1)}, f32[768]{0:T(1024)}, u32[]{:S(2)}) copy-start(f32[768]{0:T(1024)} %param.23) | copy-start | bytes 9220
  215.5 298.3 %all-reduce.12.cloned.1.call-start = ((), (), s32[]{:S(2)}) async-start(), calls=%async_computation.10 | async-start | bytes 50331648 | tf_op jit(solution)/shard_map/psum | solution.py:168
  215.6 90.2 %collective-permute-start.6 = (bf16[512,768]{1,0:T(8,128)(2,1)}, bf16[512,768]{1,0:T(8,128)(2,1)}, u32[]{:S(2)}, u32[]{:S(2)}) collective-permute-start(bf16[512,768]{1,0:T(8,128)(2,1)} %param.31), channel_id=1, source_target_pairs={{0,2},{2,4},{4,6},{6,0},{1,3},{3,5},{5,7},{7,1},{8,10},{10,12},{12... | collective-permute-start | bytes 2359304 | tf_op jit(solution)/shard_map/ppermute | solution.py:27
  302.9 21.4 %collective-permute-start.3 = (bf16[512,768]{1,0:T(8,128)(2,1)S(1)}, bf16[512,768]{1,0:T(8,128)(2,1)S(1)}, u32[]{:S(2)}, u32[]{:S(2)}) collective-permute-start(bf16[512,768]{1,0:T(8,128)(2,1)S(1)} %multiply_convert_fusion.3), channel_id=1, source_target_pairs={{0,2},{2,4},{4,6},{6,0},{1,3},{3,5},{5,7},{7,1},{8,10},{10,12},{12... | collective-permute-start | bytes 2359304 | tf_op jit(solution)/shard_map/ppermute | solution.py:27
  304.4 36.7 %collective-permute-start.8 = (bf16[512,768]{1,0:T(8,128)(2,1)}, bf16[512,768]{1,0:T(8,128)(2,1)S(1)}, u32[]{:S(2)}, u32[]{:S(2)}) collective-permute-start(bf16[512,768]{1,0:T(8,128)(2,1)} %param.31), channel_id=1, source_target_pairs={{0,6},{2,0},{4,2},{6,4},{1,7},{3,1},{5,3},{7,5},{8,14},{10,8},{12,... | collective-permute-start | bytes 2359304 | tf_op jit(solution)/shard_map/ppermute | solution.py:30
  305.8 52.1 %collective-permute-start.7 = (bf16[512,768]{1,0:T(8,128)(2,1)}, bf16[512,768]{1,0:T(8,128)(2,1)S(1)}, u32[]{:S(2)}, u32[]{:S(2)}) collective-permute-start(bf16[512,768]{1,0:T(8,128)(2,1)} %collective-permute-done.6), channel_id=1, source_target_pairs={{0,2},{2,4},{4,6},{6,0},{1,3},{3,5},{5,7},{7,1},{8,10},{10,12},{12... | collective-permute-start | bytes 2359304 | tf_op jit(solution)/shard_map/ppermute | solution.py:27
  306.7 113.0 %copy-start.48 = (bf16[768,2048]{1,0:T(8,128)(2,1)}, bf16[768,2048]{1,0:T(8,128)(2,1)S(1)}, u32[]{:S(2)}) copy-start(bf16[768,2048]{1,0:T(8,128)(2,1)S(1)} %constant_dynamic-update-slice_fusion.2) | copy-start | bytes 9437188
  306.8 73.2 %collective-permute-start.5 = (bf16[512,768]{1,0:T(8,128)(2,1)S(1)}, bf16[512,768]{1,0:T(8,128)(2,1)S(1)}, u32[]{:S(2)}, u32[]{:S(2)}) collective-permute-start(bf16[512,768]{1,0:T(8,128)(2,1)S(1)} %multiply_convert_fusion.3), channel_id=1, source_target_pairs={{0,6},{2,0},{4,2},{6,4},{1,7},{3,1},{5,3},{7,5},{8,14},{10,8},{12,... | collective-permute-start | bytes 2359304 | tf_op jit(solution)/shard_map/ppermute | solution.py:30
  324.2 66.6 %collective-permute-start.4 = (bf16[512,768]{1,0:T(8,128)(2,1)S(1)}, bf16[512,768]{1,0:T(8,128)(2,1)S(1)}, u32[]{:S(2)}, u32[]{:S(2)}) collective-permute-start(bf16[512,768]{1,0:T(8,128)(2,1)S(1)} %collective-permute-done.3), channel_id=1, source_target_pairs={{0,2},{2,4},{4,6},{6,0},{1,3},{3,5},{5,7},{7,1},{8,10},{10,12},{12... | collective-permute-start | bytes 2359304 | tf_op jit(solution)/shard_map/ppermute | solution.py:27
  374.0 5.9 copy-start.37
  431.0 179.4 %reduce-scatter.9.cloned.1.call-start = ((), (), s32[]{:S(2)}) async-start(), calls=%async_computation.7 | async-start | bytes 7864320 | tf_op jit(solution)/shard_map/reduce_scatter | solution.py:172
  513.8 16.5 %copy-start.49 = (bf16[768,2048]{1,0:T(8,128)(2,1)S(1)}, bf16[768,2048]{1,0:T(8,128)(2,1)}, u32[]{:S(2)}) copy-start(bf16[768,2048]{1,0:T(8,128)(2,1)} %copy-done.48) | copy-start | bytes 9437188
  538.9 144.4 %reduce-scatter.7.cloned.1.call-start = ((), (), s32[]{:S(2)}) async-start(), calls=%async_computation.6 | async-start | bytes 7864320 | tf_op jit(solution)/shard_map/reduce_scatter | solution.py:172
  547.5 486.9 %reduce-scatter.11.cloned.1.call-start = ((), (), s32[]{:S(2)}) async-start(), calls=%async_computation.8 | async-start | bytes 7864320 | tf_op jit(solution)/shard_map/reduce_scatter | solution.py:172
  610.4 72.9 %copy-start.29 = (f32[512,768]{1,0:T(8,128)S(1)}, f32[512,768]{1,0:T(8,128)}, u32[]{:S(2)}) copy-start(f32[512,768]{1,0:T(8,128)} %reduce-scatter.9.cloned.1.call-done) | copy-start | bytes 4718596
  687.5 21.5 %collective-permute-start.9 = (bf16[512,768]{1,0:T(8,128)(2,1)}, bf16[512,768]{1,0:T(8,128)(2,1)S(1)}, u32[]{:S(2)}, u32[]{:S(2)}) collective-permute-start(bf16[512,768]{1,0:T(8,128)(2,1)} %get-tuple-element.442), channel_id=1, source_target_pairs={{0,2},{2,4},{4,6},{6,0},{1,3},{3,5},{5,7},{7,1},{8,10},{10,12},{12... | collective-permute-start | bytes 2359304 | tf_op jit(solution)/shard_map/ppermute | solution.py:27
  688.9 36.9 %collective-permute-start.11 = (bf16[512,768]{1,0:T(8,128)(2,1)}, bf16[512,768]{1,0:T(8,128)(2,1)S(1)}, u32[]{:S(2)}, u32[]{:S(2)}) collective-permute-start(bf16[512,768]{1,0:T(8,128)(2,1)} %get-tuple-element.442), channel_id=1, source_target_pairs={{0,6},{2,0},{4,2},{6,4},{1,7},{3,1},{5,3},{7,5},{8,14},{10,8},{12,... | collective-permute-start | bytes 2359304 | tf_op jit(solution)/shard_map/ppermute | solution.py:30
  709.0 32.4 %collective-permute-start.10 = (bf16[512,768]{1,0:T(8,128)(2,1)S(1)}, bf16[512,768]{1,0:T(8,128)(2,1)S(1)}, u32[]{:S(2)}, u32[]{:S(2)}) collective-permute-start(bf16[512,768]{1,0:T(8,128)(2,1)S(1)} %collective-permute-done.9), channel_id=1, source_target_pairs={{0,2},{2,4},{4,6},{6,0},{1,3},{3,5},{5,7},{7,1},{8,10},{10,12},{12... | collective-permute-start | bytes 2359304 | tf_op jit(solution)/shard_map/ppermute | solution.py:27
  709.6 52.3 %copy-start.52 = (bf16[384,768]{1,0:T(8,128)(2,1)S(1)}, bf16[384,768]{1,0:T(8,128)(2,1)}, u32[]{:S(2)}) copy-start(bf16[384,768]{1,0:T(8,128)(2,1)} %param.27) | copy-start | bytes 1769476
  778.9 8.8 copy-start.9
  778.9 8.8 copy-start.13
  778.9 8.8 copy-start.60
  789.1 6.4 copy-start.2
  826.1 6.4 copy-start.2
  866.3 9.8 copy-start.7
  866.3 9.8 copy-start.11
  866.3 9.8 copy-start.17
  866.3 9.8 copy-start.63
  877.5 5.0 copy-start.3
  905.3 5.8 copy-start.18
  940.2 6.0 copy-start.18
  946.2 6.4 copy-start.21
  946.2 6.4 copy-start.23
  958.2 6.0 copy-start.50
  964.3 514.3 %all-reduce.10.cloned.1.call-start = ((), (), s32[]{:S(2)}) async-start(), calls=%async_computation.9 | async-start | bytes 25952256 | tf_op jit(solution)/shard_map/psum | solution.py:247
  964.3 8.5 copy-start.31
  964.3 8.5 copy-start.33
  964.3 8.5 copy-start.39
  972.8 9.1 copy-start.41
  972.8 9.1 copy-start.42
  972.8 9.1 copy-start.43
  989.0 45.5 %copy-start.15 = (bf16[512,768]{1,0:T(8,128)(2,1)S(1)}, bf16[512,768]{1,0:T(8,128)(2,1)}, u32[]{:S(2)}) copy-start(bf16[512,768]{1,0:T(8,128)(2,1)} %param.21) | copy-start | bytes 2359300
  989.0 45.5 %copy-start.65 = (f32[768]{0:T(1024)S(1)}, f32[768]{0:T(1024)}, u32[]{:S(2)}) copy-start(f32[768]{0:T(1024)} %param.22) | copy-start | bytes 9220
  989.0 45.5 %copy-start.67 = (f32[512]{0:T(512)S(1)}, f32[512]{0:T(512)}, u32[]{:S(2)}) copy-start(f32[512]{0:T(512)} %copy-done.66) | copy-start | bytes 6148
  989.0 50.1 %copy-start.68 = (f32[768]{0:T(1024)S(1)}, f32[768]{0:T(1024)}, u32[]{:S(2)}) copy-start(f32[768]{0:T(1024)} %get-tuple-element.362) | copy-start | bytes 9220
  989.0 94.7 %copy-start.69 = (f32[512]{0:T(512)S(1)}, f32[512]{0:T(512)}, u32[]{:S(2)}) copy-start(f32[512]{0:T(512)} %get-tuple-element.480) | copy-start | bytes 6148
  1034.5 49.2 %copy-start.28 = (f32[512,768]{1,0:T(8,128)S(1)}, f32[512,768]{1,0:T(8,128)}, u32[]{:S(2)}) copy-start(f32[512,768]{1,0:T(8,128)} %reduce-scatter.11.cloned.1.call-done) | copy-start | bytes 4718596
  (38 other events, 103.6 us)
Sparse Core Ops, SparseCore 0:
  91.0 32.7 all-reduce.7
  215.6 82.5 reduce-scatter.4
  431.2 82.6 all-reduce.11
  539.1 71.2 reduce-scatter.8
  613.2 70.0 reduce-scatter.6
  964.4 70.0 reduce-scatter.10
  1038.5 440.0 all-reduce.9
